TPU v7x, 32 devices: a whole 2x2x4 slice. The times are simulated.
32 devices in a mesh: zero: 8 (over y, x, core), width: 4 (over z).
Axes of the slice: x: 2, y: 2, z: 4, core: 2. Of those that a mesh axis runs over, the one named last changes fastest.
Arguments:
- train_query: bfloat16 [4608, 4096], P('zero', 'width'), may hold values from -0.09375 to 0.09375
- low_query: bfloat16 [4608, 64], P('zero'), may hold values from -0.09375 to 0.09375
- high_query: bfloat16 [64, 4096], P(None, 'width'), may hold values from -0.75 to 0.75
- train_key: bfloat16 [4608, 2048], P('zero', 'width'), may hold values from -0.09375 to 0.09375
- low_key: bfloat16 [4608, 64], P('zero'), may hold values from -0.09375 to 0.09375
- high_key: bfloat16 [64, 2048], P(None, 'width'), may hold values from -0.75 to 0.75
- train_value: bfloat16 [4608, 2048], P('zero', 'width'), may hold values from -0.09375 to 0.09375
- low_value: bfloat16 [4608, 64], P('zero'), may hold values from -0.09375 to 0.09375
- high_value: bfloat16 [64, 2048], P(None, 'width'), may hold values from -0.75 to 0.75
- train_mixed: bfloat16 [4096, 4608], P('width', 'zero'), may hold values from -0.09375 to 0.09375
- low_mixed: bfloat16 [4096, 64], P('width'), may hold values from -0.09375 to 0.09375
- high_mixed: bfloat16 [64, 4608], P(None, 'zero'), may hold values from -0.75 to 0.75
- norm_train: float32 [4608], P(('zero', 'width')), may hold values from 0.25 to 1.75
- norm_step: float32 [4608], P(('zero', 'width')), may hold values from -0.3 to 0.3
Outputs:
- final_query: bfloat16 [4608, 4096], P(None, 'width')
- final_key: bfloat16 [4608, 2048], P(None, 'width')
- final_value: bfloat16 [4608, 2048], P(None, 'width')
- final_mixed: bfloat16 [4096, 4608], P('width')
- serve_norm: bfloat16 [4608], replicated
All inputs are finite; a program needn't handle non-finite values.
Results may differ from a plain program's by a relative error of at most 0.001.
Values may be sent and summed in bfloat16 or wider, within the bound.
No kernel may reach another device: no remote copies, remote signals or barrier semaphores. Data moves between devices by JAX's collectives and lax.ppermute only.
A program may use at most 192 MiB of HBM per device.

v0:
```python
import math

import jax
import jax.numpy as jnp
from jax import lax
from jax.experimental import pallas as pl
from jax.experimental.pallas import tpu as pltpu
from jax.sharding import PartitionSpec as P


mix_rate = 0.5


def merged(train, low, high):
    update = jnp.dot(low, high, preferred_element_type=jnp.float32)
    return (train.astype(jnp.float32) + mix_rate * update).astype(jnp.bfloat16)


def place(targets, moves, offsets, shapes):
    pieces = [move[0] for move in moves]
    count = len(pieces)
    kept = [index for index, target in enumerate(targets) if target is not None]

    def body(offsets_ref, *refs):
        sources = refs[:count]
        outputs = refs[count + len(kept) : count + len(kept) + len(shapes)]
        stages = refs[-count - 2 : -2]
        arrivals, departures = refs[-2:]
        loads, stores = [], []
        for index, (piece, output, row, column) in enumerate(moves):
            rows = pl.ds(pl.multiple_of(offsets_ref[row], 16), piece.shape[0])
            columns = pl.ds(pl.multiple_of(offsets_ref[column], 128), piece.shape[1])
            loads.append(
                pltpu.make_async_copy(sources[index], stages[index], arrivals.at[index])
            )
            stores.append(
                pltpu.make_async_copy(
                    stages[index], outputs[output].at[rows, columns], departures.at[index]
                )
            )
        for load in loads:
            load.start()
        for load, store in zip(loads, stores):
            load.wait()
            store.start()
        for store in stores:
            store.wait()

    anywhere = pl.BlockSpec(memory_space=pl.ANY)
    return pl.pallas_call(
        body,
        out_shape=[jax.ShapeDtypeStruct(shape, jnp.bfloat16) for shape in shapes],
        in_specs=[pl.BlockSpec(memory_space=pltpu.SMEM)] + [anywhere] * (count + len(kept)),
        out_specs=[anywhere] * len(shapes),
        scratch_shapes=[pltpu.VMEM(piece.shape, piece.dtype) for piece in pieces]
        + [pltpu.SemaphoreType.DMA((count,)), pltpu.SemaphoreType.DMA((count,))],
        input_output_aliases={1 + count + place_: index for place_, index in enumerate(kept)},
        compiler_params=pltpu.CompilerParams(vmem_limit_bytes=40 * 2**20),
    )(offsets, *pieces, *[targets[index] for index in kept])


def solution(mesh):
    zero, width = mesh.shape["zero"], mesh.shape["width"]
    cores = 2 if zero % 2 == 0 else 1
    chips = zero // cores
    side_y = max(n for n in range(1, math.isqrt(chips) + 1) if chips % n == 0)
    side_x = chips // side_y

    def number(y, x, core):
        return ((y % side_y) * side_x + x % side_x) * cores + core % cores

    def shift(value, dy=0, dx=0, dcore=0):
        pairs = [
            (number(y + dy, x + dx, core + dcore), number(y, x, core))
            for y in range(side_y)
            for x in range(side_x)
            for core in range(cores)
        ]
        return lax.ppermute(value, "zero", pairs)

    def gather_norm(norm, y, x, core):
        around = [norm]
        for step in range(1, width):
            pairs = [((z + step) % width, z) for z in range(width)]
            around.append(lax.ppermute(norm, "width", pairs))
        gathered = jnp.roll(jnp.stack(around), lax.axis_index("width"), axis=0)
        around = [gathered]
        for step in range(1, cores):
            around.append(shift(gathered, dcore=step))
        gathered = jnp.roll(jnp.stack(around), core, axis=0)
        around = []
        for dy in range(side_y):
            for dx in range(side_x):
                if dy == 0 and dx == 0:
                    around.append(gathered)
                else:
                    around.append(shift(gathered, dy=dy, dx=dx))
        around = jnp.stack(around).reshape(side_y, side_x, -1)
        return jnp.roll(around, (y, x), axis=(0, 1)).reshape(-1)

    corner = (side_y - 1, side_x - 1)
    spots = [(dy, dx) for dy in range(side_y) for dx in range(side_x)]
    groups = [
        [(output, (0, 0)) for output in range(4)]
        + [(output, spot) for output in (0, 1) for spot in spots if spot[0] == 0 and spot[1] > 0]
        + [(output, spot) for output in (2, 3) for spot in spots if spot[1] == 0 and spot[0] > 0],
    ]
    rest = [(output, spot) for output in range(4) for spot in spots if (output, spot) not in groups[0]]
    groups += [
        [(output, spot) for output, spot in rest if spot != corner],
        [(output, spot) for output, spot in rest if spot == corner and output in (0, 3)],
        [(output, spot) for output, spot in rest if spot == corner and output in (1, 2)],
    ]

    def on_device(
        train_query,
        low_query,
        high_query,
        train_key,
        low_key,
        high_key,
        train_value,
        low_value,
        high_value,
        train_mixed,
        low_mixed,
        high_mixed,
        norm_train,
        norm_step,
    ):
        norm = (norm_train + norm_step).astype(jnp.bfloat16)
        key = merged(train_key, low_key, high_key)
        mixed = merged(train_mixed, low_mixed, high_mixed)
        value = merged(train_value, low_value, high_value)
        query = merged(train_query, low_query, high_query)
        rows, columns = query.shape[0], mixed.shape[1]
        aligned = rows % 16 == 0 and (cores * columns) % 128 == 0
        aligned = aligned and mixed.shape[0] % (16 * cores) == 0
        if not aligned or cores == 1:
            return (
                lax.all_gather(query, "zero", axis=0, tiled=True),
                lax.all_gather(key, "zero", axis=0, tiled=True),
                lax.all_gather(value, "zero", axis=0, tiled=True),
                lax.all_gather(mixed, "zero", axis=1, tiled=True),
                lax.all_gather(norm, ("zero", "width"), axis=0, tiled=True),
            )

        index = lax.axis_index("zero")
        core = index % cores
        x = (index // cores) % side_x
        y = index // (cores * side_x)

        other_mixed = shift(mixed, dcore=1)
        pair = jnp.where(
            core == 0,
            jnp.concatenate([mixed, other_mixed], axis=1),
            jnp.concatenate([other_mixed, mixed], axis=1),
        )
        half = mixed.shape[0] // cores
        mixed_part = lax.dynamic_slice_in_dim(pair, core * half, half, axis=0)

        def x_first(own):
            held = {(0, 0): own}
            for dx in range(1, side_x):
                held[0, dx] = shift(held[0, dx - 1], dx=1)
            for dy in range(1, side_y):
                for dx in range(side_x):
                    held[dy, dx] = shift(held[dy - 1, dx], dy=1)
            return held

        def y_first(own):
            held = {(0, 0): own}
            for dy in range(1, side_y):
                held[dy, 0] = shift(held[dy - 1, 0], dy=1)
            for dx in range(1, side_x):
                for dy in range(side_y):
                    held[dy, dx] = shift(held[dy, dx - 1], dx=1)
            return held

        keys, queries = x_first(key), x_first(query)
        values, mixeds = y_first(value), y_first(mixed_part)

        offsets = [jnp.zeros_like(index), core * half, (1 - core) * half]
        slots = {}
        for dy in range(side_y):
            for dx in range(side_x):
                chip = ((y + dy) % side_y) * side_x + (x + dx) % side_x
                slots[dy, dx] = len(offsets)
                offsets += [
                    (chip * cores + core) * rows,
                    (chip * cores + 1 - core) * rows,
                    chip * (cores * columns),
                ]
        offsets = jnp.stack(offsets).astype(jnp.int32)

        def moves_of(held, output, spot):
            piece, slot = held[spot], slots[spot]
            if output == 3:
                if spot == (0, 0):
                    return [(pair, 3, 0, slot + 2)]
                return [
                    (piece, 3, 1, slot + 2),
                    (shift(piece, dcore=1), 3, 2, slot + 2),
                ]
            return [
                (piece, output, slot, 0),
                (shift(piece, dcore=1), output, slot + 1, 0),
            ]

        shapes = [
            (rows * zero, query.shape[1]),
            (rows * zero, key.shape[1]),
            (rows * zero, value.shape[1]),
            (mixed.shape[0], columns * zero),
        ]
        held_of = (queries, keys, values, mixeds)
        outputs = [None] * 4
        for group in groups:
            moves = [move for output, spot in group for move in moves_of(held_of[output], output, spot)]
            outputs = place(outputs, moves, offsets, shapes)
        return (*outputs, gather_norm(norm, y, x, core))

    return jax.shard_map(
        on_device,
        mesh=mesh,
        in_specs=(
            P("zero", "width"),
            P("zero", None),
            P(None, "width"),
            P("zero", "width"),
            P("zero", None),
            P(None, "width"),
            P("zero", "width"),
            P("zero", None),
            P(None, "width"),
            P("width", "zero"),
            P("width", None),
            P(None, "zero"),
            P(("zero", "width")),
            P(("zero", "width")),
        ),
        out_specs=(P(None, "width"), P(None, "width"), P(None, "width"), P("width", None), P()),
        check_vma=False,
    )
```

profile of v0, /device:TPU:0, one launch (start us, length us, event | category | flops | bytes accessed | tf_op | source)
XLA Modules:
  0.0 188.3 jit_solution(10304843052887582053)
XLA Ops:
  0.7 0.7 add_convert_fusion.2
  1.4 5.1 %collective-permute-start.28 = (bf16[144]{0:T(256)(128)(2,1)S(1)}, bf16[144]{0:T(256)(128)(2,1)S(1)}, u32[]{:S(2)}, u32[]{:S(2)}) collective-permute-start(bf16[144]{0:T(256)(128)(2,1)S(1)} %add_convert_fusion.2), channel_id=1, source_target_pairs={{1,0},{2,1},{3,2},{0,3},{5,4},{6,5},{7,6},{4,7},{9,8},{10,9},{11,1... | collective-permute-start | bytes 872 | tf_op jit(solution)/shard_map/ppermute | solution.py:85
  6.5 1.0 collective-permute-start.30
  7.5 2.8 %copy.39 = f32[1024,576]{1,0:T(8,128)} copy(bf16[1024,576]{0,1:T(8,128)(2,1)} %param.23) | data formatting | bytes 3538944 | tf_op jit(solution)/shard_map/convert_element_type | solution.py:16
  10.3 2.3 %add_convert_fusion = bf16[1024,576]{1,0:T(8,128)(2,1)S(1)} fusion(f32[1024,576]{1,0:T(8,128)} %copy.39, bf16[1024,64]{0,1:T(8,128)(2,1)S(1)} %copy-done, bf16[64,576]{1,0:T(8,128)(2,1)S(1)} %copy-done.33), kind=kOutput, calls=%fused_computation | convolution fusion | flops 77266944 | bytes 3743744 | tf_op jit(solution)/shard_map/dot_general | solution.py:15
  12.7 1.4 copy.40
  14.2 1.2 fusion.3.refs_2_
  15.3 1.5 collective-permute-start
  16.9 0.3 collective-permute-start.31
  17.2 0.9 collective-permute-done.31
  18.2 0.7 collective-permute-start.32
  18.9 1.5 collective-permute-start.33
  20.4 1.3 collective-permute-start.34
  21.8 1.2 fusion.2.refs_4_
  22.9 8.5 %collective-permute-done.32 = bf16[2,4,144]{2,1,0:T(4,128)(2,1)S(1)} collective-permute-done((bf16[2,4,144]{2,1,0:T(4,128)(2,1)S(1)}, bf16[2,4,144]{2,1,0:T(4,128)(2,1)S(1)}, u32[]{:S(2)}, u32[]{:S(2)}) %collective-permute-start.32) | collective-permute-done | bytes 2336 | tf_op jit(solution)/shard_map/ppermute | solution.py:79
  31.4 1.5 collective-permute-start.3
  32.9 0.2 collective-permute-start.23
  33.2 1.9 add_convert_fusion.1.refs_0_
  35.1 1.6 collective-permute-start.6
  36.6 10.7 %collective-permute-done.3.refs_11_ = bf16[576,512]{1,0:T(8,128)(2,1)S(1)} collective-permute-done((bf16[576,512]{1,0:T(8,128)(2,1)}, bf16[576,512]{1,0:T(8,128)(2,1)S(1)}, u32[]{:S(2)}, u32[]{:S(2)}) %collective-permute-start.3) | collective-permute-done | bytes 589856 | tf_op jit(solution)/shard_map/ppermute | solution.py:79
  47.4 1.5 collective-permute-start.15
  48.9 1.5 collective-permute-start.17
  50.4 2.4 %copy.41 = bf16[1024,576]{1,0:T(8,128)(2,1)} copy(bf16[1024,576]{0,1:T(8,128)(2,1)} %collective-permute-done.9) | data formatting | bytes 2359296 | tf_op jit(solution)/shard_map/ppermute | solution.py:79
  52.8 0.8 copy-done.9
  53.6 0.8 copy-done.14
  54.4 0.5 collective-permute-start.13
  55.0 5.1 %maximum_select_fusion.refs_6_ = bf16[1024,1152]{1,0:T(8,128)(2,1)S(1)} fusion(bf16[1024,576]{1,0:T(8,128)(2,1)} %copy.41, bf16[1024,576]{1,0:T(8,128)(2,1)} %copy-done.28, pred[]{:T(512)S(6)} %eq.23), kind=kLoop, calls=%fused_computation.1 | loop fusion | flops 10616832 | bytes 4718593 | tf_op jit(solution)/shard_map/jit(_where)/select_n | solution.py:154
  60.1 3.8 %collective-permute-done.15.refs_2_ = bf16[576,512]{1,0:T(8,128)(2,1)} collective-permute-done((bf16[576,512]{1,0:T(8,128)(2,1)}, bf16[576,512]{1,0:T(8,128)(2,1)}, u32[]{:S(2)}, u32[]{:S(2)}) %collective-permute-start.15) | collective-permute-done | bytes 589856 | tf_op jit(solution)/shard_map/ppermute | solution.py:79
  63.9 12.1 %collective-permute-done.17.refs_4_ = bf16[576,512]{1,0:T(8,128)(2,1)} collective-permute-done((bf16[576,512]{1,0:T(8,128)(2,1)}, bf16[576,512]{1,0:T(8,128)(2,1)}, u32[]{:S(2)}, u32[]{:S(2)}) %collective-permute-start.17) | collective-permute-done | bytes 589856 | tf_op jit(solution)/shard_map/ppermute | solution.py:79
  76.2 0.6 collective-permute-start.10
  76.7 0.8 copy-done.16
  77.8 0.3 collective-permute-done.26.refs_12_
  78.0 0.8 copy-done.18
  79.0 1.0 copy-done.2
  80.0 0.4 collective-permute-start.18
  80.4 8.8 %collective-permute-done.13.refs_0_ = bf16[576,1024]{1,0:T(8,128)(2,1)} collective-permute-done((bf16[576,1024]{1,0:T(8,128)(2,1)S(1)}, bf16[576,1024]{1,0:T(8,128)(2,1)}, u32[]{:S(2)}, u32[]{:S(2)}) %collective-permute-start.13) | collective-permute-done | bytes 1179680 | tf_op jit(solution)/shard_map/ppermute | solution.py:79
  89.2 1.5 collective-permute-start.1
  90.7 0.8 copy-done.24
  91.5 1.5 collective-permute-start.4
  93.0 0.8 copy-done.26
  93.8 0.5 collective-permute-start.19
  94.4 31.4 %collective-permute-done.1.refs_0_ = bf16[576,512]{1,0:T(8,128)(2,1)S(1)} collective-permute-done((bf16[576,512]{1,0:T(8,128)(2,1)S(1)}, bf16[576,512]{1,0:T(8,128)(2,1)S(1)}, u32[]{:S(2)}, u32[]{:S(2)}) %collective-permute-start.1) | collective-permute-done | bytes 589856 | tf_op jit(solution)/shard_map/ppermute | solution.py:79
  125.8 1.5 collective-permute-start.7
  127.3 1.5 collective-permute-start.11
  128.8 1.1 copy-done.4
  129.9 0.4 collective-permute-start.27
  130.4 22.5 %collective-permute-done.7.refs_0_ = bf16[576,1024]{1,0:T(8,128)(2,1)} collective-permute-done((bf16[576,1024]{1,0:T(8,128)(2,1)}, bf16[576,1024]{1,0:T(8,128)(2,1)}, u32[]{:S(2)}, u32[]{:S(2)}) %collective-permute-start.7) | collective-permute-done | bytes 1179680 | tf_op jit(solution)/shard_map/ppermute | solution.py:79
  153.0 1.9 collective-permute-done.11.refs_2_
  154.9 0.6 collective-permute-start.2
  155.6 1.3 pad_maximum_fusion
  156.9 0.8 reshape.16
  157.9 0.6 reshape.17
  158.5 1.3 copy-done.3
  159.7 1.3 copy-done.5
  161.0 1.1 copy-done.8
  162.1 1.1 copy-done.10
  163.1 1.1 copy-done.13
  164.2 1.1 copy-done.15
  165.3 1.1 copy-done.17
  166.3 1.1 copy-done.19
  167.4 7.7 %shard_map.173 = (bf16[4608,1024]{1,0:T(8,128)(2,1)}, bf16[4608,512]{1,0:T(8,128)(2,1)}, bf16[4608,512]{1,0:T(8,128)(2,1)}, bf16[1024,4608]{1,0:T(8,128)(2,1)}) custom-call(s32[15]{0:T(128)S(1)} %stack.94.offsets_ref, bf16[576,1024]{1,0:T(8,128)(2,1)S(1)} %add_convert_fusion.1.refs_0_, bf16[576,1024]{1,0:T(8,128)(2,1)S(1)} %copy-done.3, ...), custom_call_target="tpu_custom_call" | custom-call | tf_op jit(solution)/shard_map/pallas_call | solution.py:50
  175.2 5.6 %shard_map.174 = (bf16[4608,1024]{1,0:T(8,128)(2,1)}, bf16[4608,512]{1,0:T(8,128)(2,1)}, bf16[4608,512]{1,0:T(8,128)(2,1)}, bf16[1024,4608]{1,0:T(8,128)(2,1)}) custom-call(s32[15]{0:T(128)S(1)} %stack.94.offsets_ref, bf16[576,1024]{1,0:T(8,128)(2,1)} %collective-permute-done.13.refs_0_, ...), custom_call_target="tpu_custom_call", output_to_operand_aliasing={{0}: (9, {}), {1}: (10, {}), {2}: (11, {}), {3}: (12, {})} | custom-call | tf_op jit(solution)/shard_map/pallas_call | solution.py:50
  180.9 4.3 %shard_map.175 = (bf16[4608,1024]{1,0:T(8,128)(2,1)}, bf16[4608,512]{1,0:T(8,128)(2,1)}, bf16[4608,512]{1,0:T(8,128)(2,1)}, bf16[1024,4608]{1,0:T(8,128)(2,1)}) custom-call(s32[15]{0:T(128)S(1)} %stack.94.offsets_ref, bf16[576,1024]{1,0:T(8,128)(2,1)} %collective-permute-done.7.refs_0_, ...), custom_call_target="tpu_custom_call", output_to_operand_aliasing={{0}: (5, {}), {1}: (6, {}), {2}: (7, {}), {3}: (8, {})} | custom-call | tf_op jit(solution)/shard_map/pallas_call | solution.py:50
  185.2 3.1 %shard_map.176 = (bf16[4608,1024]{1,0:T(8,128)(2,1)}, bf16[4608,512]{1,0:T(8,128)(2,1)}, bf16[4608,512]{1,0:T(8,128)(2,1)}, bf16[1024,4608]{1,0:T(8,128)(2,1)}) custom-call(s32[15]{0:T(128)S(1)} %stack.94.offsets_ref, bf16[576,512]{1,0:T(8,128)(2,1)S(1)} %copy-done.21, ...), custom_call_target="tpu_custom_call", output_to_operand_aliasing={{0}: (5, {}), {1}: (6, {}), {2}: (7, {}), {3}: (8, {})} | custom-call | tf_op jit(solution)/shard_map/pallas_call | solution.py:50
  (107 shorter events, 1.2 us)
Async XLA Ops:
  0.6 9.7 %copy-start = (bf16[1024,64]{0,1:T(8,128)(2,1)S(1)}, bf16[1024,64]{0,1:T(8,128)(2,1)}, u32[]{:S(2)}) copy-start(bf16[1024,64]{0,1:T(8,128)(2,1)} %param.24) | copy-start | bytes 393220
  0.6 9.6 %copy-start.33 = (bf16[64,576]{1,0:T(8,128)(2,1)S(1)}, bf16[64,576]{1,0:T(8,128)(2,1)}, u32[]{:S(2)}) copy-start(bf16[64,576]{1,0:T(8,128)(2,1)} %param.25) | copy-start | bytes 221188
  1.4 15.4 %collective-permute-start.28 = (bf16[144]{0:T(256)(128)(2,1)S(1)}, bf16[144]{0:T(256)(128)(2,1)S(1)}, u32[]{:S(2)}, u32[]{:S(2)}) collective-permute-start(bf16[144]{0:T(256)(128)(2,1)S(1)} %add_convert_fusion.2), channel_id=1, source_target_pairs={{1,0},{2,1},{3,2},{0,3},{5,4},{6,5},{7,6},{4,7},{9,8},{10,9},{11,1... | collective-permute-start | bytes 872 | tf_op jit(solution)/shard_map/ppermute | solution.py:85
  6.5 10.4 %collective-permute-start.29 = (bf16[144]{0:T(256)(128)(2,1)S(1)}, bf16[144]{0:T(256)(128)(2,1)S(1)}, u32[]{:S(2)}, u32[]{:S(2)}) collective-permute-start(bf16[144]{0:T(256)(128)(2,1)S(1)} %add_convert_fusion.2), channel_id=1, source_target_pairs={{2,0},{3,1},{0,2},{1,3},{6,4},{7,5},{4,6},{5,7},{10,8},{11,9},{8,1... | collective-permute-start | bytes 872 | tf_op jit(solution)/shard_map/ppermute | solution.py:85
  6.5 10.4 %collective-permute-start.30 = (bf16[144]{0:T(256)(128)(2,1)S(1)}, bf16[144]{0:T(256)(128)(2,1)S(1)}, u32[]{:S(2)}, u32[]{:S(2)}) collective-permute-start(bf16[144]{0:T(256)(128)(2,1)S(1)} %add_convert_fusion.2), channel_id=1, source_target_pairs={{3,0},{0,1},{1,2},{2,3},{7,4},{4,5},{5,6},{6,7},{11,8},{8,9},{9,10... | collective-permute-start | bytes 872 | tf_op jit(solution)/shard_map/ppermute | solution.py:85
  10.3 3.9 %copy-start.29 = (bf16[576,512]{1,0:T(8,128)(2,1)S(1)}, bf16[576,512]{1,0:T(8,128)(2,1)}, u32[]{:S(2)}) copy-start(bf16[576,512]{1,0:T(8,128)(2,1)} %param.17) | copy-start | bytes 1769476
  10.3 3.9 %copy-start.31 = (bf16[576,64]{0,1:T(8,128)(2,1)S(1)}, bf16[576,64]{0,1:T(8,128)(2,1)}, u32[]{:S(2)}) copy-start(bf16[576,64]{0,1:T(8,128)(2,1)} %param.18) | copy-start | bytes 221188
  10.3 3.9 %copy-start.34 = (bf16[64,512]{1,0:T(8,128)(2,1)S(1)}, bf16[64,512]{1,0:T(8,128)(2,1)}, u32[]{:S(2)}) copy-start(bf16[64,512]{1,0:T(8,128)(2,1)} %param.19) | copy-start | bytes 196612
  12.7 1.5 copy-start.28
  12.7 9.1 %copy-start.30 = (bf16[576,512]{1,0:T(8,128)(2,1)S(1)}, bf16[576,512]{1,0:T(8,128)(2,1)}, u32[]{:S(2)}) copy-start(bf16[576,512]{1,0:T(8,128)(2,1)} %param.20) | copy-start | bytes 1769476
  12.7 9.1 %copy-start.32 = (bf16[576,64]{0,1:T(8,128)(2,1)S(1)}, bf16[576,64]{0,1:T(8,128)(2,1)}, u32[]{:S(2)}) copy-start(bf16[576,64]{0,1:T(8,128)(2,1)} %param.21) | copy-start | bytes 221188
  12.7 9.1 %copy-start.35 = (bf16[64,512]{1,0:T(8,128)(2,1)S(1)}, bf16[64,512]{1,0:T(8,128)(2,1)}, u32[]{:S(2)}) copy-start(bf16[64,512]{1,0:T(8,128)(2,1)} %param.22) | copy-start | bytes 196612
  14.1 34.8 %collective-permute-start.9 = (bf16[1024,576]{0,1:T(8,128)(2,1)}, bf16[1024,576]{0,1:T(8,128)(2,1)}, u32[]{:S(2)}, u32[]{:S(2)}) collective-permute-start(bf16[1024,576]{0,1:T(8,128)(2,1)} %copy.40), channel_id=1, source_target_pairs={{4,0},{0,4},{12,8},{8,12},{20,16},{16,20},{28,24},{24,28},{5,1},{1... | collective-permute-start | bytes 3538952 | tf_op jit(solution)/shard_map/ppermute | solution.py:79
  15.3 19.7 %collective-permute-start = (bf16[576,512]{1,0:T(8,128)(2,1)}, bf16[576,512]{1,0:T(8,128)(2,1)S(1)}, u32[]{:S(2)}, u32[]{:S(2)}) collective-permute-start(bf16[576,512]{1,0:T(8,128)(2,1)} %fusion.3.refs_2_), channel_id=1, source_target_pairs={{8,0},{12,4},{0,8},{4,12},{24,16},{28,20},{16,24},{20,28},{9,1},{1... | collective-permute-start | bytes 1769480 | tf_op jit(solution)/shard_map/ppermute | solution.py:79
  16.9 1.2 collective-permute-start.31
  18.2 13.2 %collective-permute-start.32 = (bf16[2,4,144]{2,1,0:T(4,128)(2,1)S(1)}, bf16[2,4,144]{2,1,0:T(4,128)(2,1)S(1)}, u32[]{:S(2)}, u32[]{:S(2)}) collective-permute-start(bf16[2,4,144]{2,1,0:T(4,128)(2,1)S(1)} %fusion.8), channel_id=1, source_target_pairs={{8,0},{12,4},{0,8},{4,12},{24,16},{28,20},{16,24},{20,28},{9,1},{1... | collective-permute-start | bytes 6920 | tf_op jit(solution)/shard_map/ppermute | solution.py:79
  18.9 12.5 %collective-permute-start.33 = (bf16[2,4,144]{2,1,0:T(4,128)(2,1)S(1)}, bf16[2,4,144]{2,1,0:T(4,128)(2,1)}, u32[]{:S(2)}, u32[]{:S(2)}) collective-permute-start(bf16[2,4,144]{2,1,0:T(4,128)(2,1)S(1)} %fusion.8), channel_id=1, source_target_pairs={{16,0},{20,4},{24,8},{28,12},{0,16},{4,20},{8,24},{12,28},{17,1},{... | collective-permute-start | bytes 6920 | tf_op jit(solution)/shard_map/ppermute | solution.py:79
  20.4 12.5 %collective-permute-start.34 = (bf16[2,4,144]{2,1,0:T(4,128)(2,1)S(1)}, bf16[2,4,144]{2,1,0:T(4,128)(2,1)}, u32[]{:S(2)}, u32[]{:S(2)}) collective-permute-start(bf16[2,4,144]{2,1,0:T(4,128)(2,1)S(1)} %fusion.8), channel_id=1, source_target_pairs={{24,0},{28,4},{16,8},{20,12},{8,16},{12,20},{0,24},{4,28},{25,1},{... | collective-permute-start | bytes 6920 | tf_op jit(solution)/shard_map/ppermute | solution.py:79
  31.4 21.4 %collective-permute-start.22 = (bf16[576,512]{1,0:T(8,128)(2,1)}, bf16[576,512]{1,0:T(8,128)(2,1)S(1)}, u32[]{:S(2)}, u32[]{:S(2)}) collective-permute-start(bf16[576,512]{1,0:T(8,128)(2,1)} %fusion.3.refs_2_), channel_id=1, source_target_pairs={{4,0},{0,4},{12,8},{8,12},{20,16},{16,20},{28,24},{24,28},{5,1},{1... | collective-permute-start | bytes 1769480 | tf_op jit(solution)/shard_map/ppermute | solution.py:79
  31.4 16.0 %collective-permute-start.3 = (bf16[576,512]{1,0:T(8,128)(2,1)}, bf16[576,512]{1,0:T(8,128)(2,1)S(1)}, u32[]{:S(2)}, u32[]{:S(2)}) collective-permute-start(bf16[576,512]{1,0:T(8,128)(2,1)} %fusion.2.refs_4_), channel_id=1, source_target_pairs={{16,0},{20,4},{24,8},{28,12},{0,16},{4,20},{8,24},{12,28},{17,1},{... | collective-permute-start | bytes 1769480 | tf_op jit(solution)/shard_map/ppermute | solution.py:79
  32.9 20.7 %collective-permute-start.23 = (bf16[576,512]{1,0:T(8,128)(2,1)}, bf16[576,512]{1,0:T(8,128)(2,1)S(1)}, u32[]{:S(2)}, u32[]{:S(2)}) collective-permute-start(bf16[576,512]{1,0:T(8,128)(2,1)} %fusion.2.refs_4_), channel_id=1, source_target_pairs={{4,0},{0,4},{12,8},{8,12},{20,16},{16,20},{28,24},{24,28},{5,1},{1... | collective-permute-start | bytes 1769480 | tf_op jit(solution)/shard_map/ppermute | solution.py:79
  35.1 18.5 %copy-start.6 = (bf16[576,512]{1,0:T(8,128)(2,1)}, bf16[576,512]{1,0:T(8,128)(2,1)S(1)}, u32[]{:S(2)}) copy-start(bf16[576,512]{1,0:T(8,128)(2,1)S(1)} %collective-permute-done.refs_9_) | copy-start | bytes 1769476
  35.1 41.1 %collective-permute-start.6 = (bf16[576,1024]{1,0:T(8,128)(2,1)S(1)}, bf16[576,1024]{1,0:T(8,128)(2,1)}, u32[]{:S(2)}, u32[]{:S(2)}) collective-permute-start(bf16[576,1024]{1,0:T(8,128)(2,1)S(1)} %add_convert_fusion.1.refs_0_), channel_id=1, source_target_pairs={{8,0},{12,4},{0,8},{4,12},{24,16},{28,20},{16,24},{20,28},{9,1},{1... | collective-permute-start | bytes 3538952 | tf_op jit(solution)/shard_map/ppermute | solution.py:79
  47.4 6.2 %copy-start.11 = (bf16[576,512]{1,0:T(8,128)(2,1)}, bf16[576,512]{1,0:T(8,128)(2,1)S(1)}, u32[]{:S(2)}) copy-start(bf16[576,512]{1,0:T(8,128)(2,1)S(1)} %collective-permute-done.3.refs_11_) | copy-start | bytes 1769476
  47.4 16.5 %collective-permute-start.15 = (bf16[576,512]{1,0:T(8,128)(2,1)}, bf16[576,512]{1,0:T(8,128)(2,1)}, u32[]{:S(2)}, u32[]{:S(2)}) collective-permute-start(bf16[576,512]{1,0:T(8,128)(2,1)} %fusion.3.refs_2_), channel_id=1, source_target_pairs={{16,0},{20,4},{24,8},{28,12},{0,16},{4,20},{8,24},{12,28},{17,1},{... | collective-permute-start | bytes 1769480 | tf_op jit(solution)/shard_map/ppermute | solution.py:79
  48.9 27.1 %collective-permute-start.17 = (bf16[576,512]{1,0:T(8,128)(2,1)}, bf16[576,512]{1,0:T(8,128)(2,1)}, u32[]{:S(2)}, u32[]{:S(2)}) collective-permute-start(bf16[576,512]{1,0:T(8,128)(2,1)} %fusion.2.refs_4_), channel_id=1, source_target_pairs={{8,0},{12,4},{0,8},{4,12},{24,16},{28,20},{16,24},{20,28},{9,1},{1... | collective-permute-start | bytes 1769480 | tf_op jit(solution)/shard_map/ppermute | solution.py:79
  53.6 25.4 %collective-permute-start.21 = (bf16[576,1024]{1,0:T(8,128)(2,1)S(1)}, bf16[576,1024]{1,0:T(8,128)(2,1)S(1)}, u32[]{:S(2)}, u32[]{:S(2)}) collective-permute-start(bf16[576,1024]{1,0:T(8,128)(2,1)S(1)} %add_convert_fusion.1.refs_0_), channel_id=1, source_target_pairs={{4,0},{0,4},{12,8},{8,12},{20,16},{16,20},{28,24},{24,28},{5,1},{1... | collective-permute-start | bytes 3538952 | tf_op jit(solution)/shard_map/ppermute | solution.py:79
  54.4 34.7 %collective-permute-start.13 = (bf16[576,1024]{1,0:T(8,128)(2,1)S(1)}, bf16[576,1024]{1,0:T(8,128)(2,1)}, u32[]{:S(2)}, u32[]{:S(2)}) collective-permute-start(bf16[576,1024]{1,0:T(8,128)(2,1)S(1)} %add_convert_fusion.1.refs_0_), channel_id=1, source_target_pairs={{16,0},{20,4},{24,8},{28,12},{0,16},{4,20},{8,24},{12,28},{17,1},{... | collective-permute-start | bytes 3538952 | tf_op jit(solution)/shard_map/ppermute | solution.py:79
  54.9 8.9 %copy-start.7 = (bf16[576,512]{1,0:T(8,128)(2,1)S(1)}, bf16[576,512]{1,0:T(8,128)(2,1)}, u32[]{:S(2)}) copy-start(bf16[576,512]{1,0:T(8,128)(2,1)} %copy-done.6) | copy-start | bytes 1769476
  55.0 21.1 %copy-start.12 = (bf16[576,512]{1,0:T(8,128)(2,1)S(1)}, bf16[576,512]{1,0:T(8,128)(2,1)}, u32[]{:S(2)}) copy-start(bf16[576,512]{1,0:T(8,128)(2,1)} %copy-done.11) | copy-start | bytes 1769476
  63.9 12.8 %collective-permute-start.25 = (bf16[576,512]{1,0:T(8,128)(2,1)S(1)}, bf16[576,512]{1,0:T(8,128)(2,1)S(1)}, u32[]{:S(2)}, u32[]{:S(2)}) collective-permute-start(bf16[576,512]{1,0:T(8,128)(2,1)S(1)} %copy-done.7), channel_id=1, source_target_pairs={{4,0},{0,4},{12,8},{8,12},{20,16},{16,20},{28,24},{24,28},{5,1},{1... | collective-permute-start | bytes 1769480 | tf_op jit(solution)/shard_map/ppermute | solution.py:79
  76.0 2.0 %collective-permute-start.26 = (bf16[576,512]{1,0:T(8,128)(2,1)S(1)}, bf16[576,512]{1,0:T(8,128)(2,1)S(1)}, u32[]{:S(2)}, u32[]{:S(2)}) collective-permute-start(bf16[576,512]{1,0:T(8,128)(2,1)S(1)} %copy-done.12), channel_id=1, source_target_pairs={{4,0},{0,4},{12,8},{8,12},{20,16},{16,20},{28,24},{24,28},{5,1},{1... | collective-permute-start | bytes 1769480 | tf_op jit(solution)/shard_map/ppermute | solution.py:79
  76.2 51.1 %collective-permute-start.10 = (bf16[512,1152]{1,0:T(8,128)(2,1)S(1)}, bf16[512,1152]{1,0:T(8,128)(2,1)}, u32[]{:S(2)}, u32[]{:S(2)}) collective-permute-start(bf16[512,1152]{1,0:T(8,128)(2,1)S(1)} %constant_dynamic-slice_fusion.1), channel_id=1, source_target_pairs={{16,0},{20,4},{24,8},{28,12},{0,16},{4,20},{8,24},{12,28},{17,1},{... | collective-permute-start | bytes 3538952 | tf_op jit(solution)/shard_map/ppermute | solution.py:79
  77.6 13.1 %collective-permute-start.16 = (bf16[576,512]{1,0:T(8,128)(2,1)}, bf16[576,512]{1,0:T(8,128)(2,1)S(1)}, u32[]{:S(2)}, u32[]{:S(2)}) collective-permute-start(bf16[576,512]{1,0:T(8,128)(2,1)} %collective-permute-done.15.refs_2_), channel_id=1, source_target_pairs={{4,0},{0,4},{12,8},{8,12},{20,16},{16,20},{28,24},{24,28},{5,1},{1... | collective-permute-start | bytes 1769480 | tf_op jit(solution)/shard_map/ppermute | solution.py:79
  78.9 49.9 %collective-permute-start.24 = (bf16[576,1024]{1,0:T(8,128)(2,1)}, bf16[576,1024]{1,0:T(8,128)(2,1)S(1)}, u32[]{:S(2)}, u32[]{:S(2)}) collective-permute-start(bf16[576,1024]{1,0:T(8,128)(2,1)} %collective-permute-done.6.refs_7_), channel_id=1, source_target_pairs={{4,0},{0,4},{12,8},{8,12},{20,16},{16,20},{28,24},{24,28},{5,1},{1... | collective-permute-start | bytes 3538952 | tf_op jit(solution)/shard_map/ppermute | solution.py:79
  80.0 13.0 %collective-permute-start.18 = (bf16[576,512]{1,0:T(8,128)(2,1)}, bf16[576,512]{1,0:T(8,128)(2,1)S(1)}, u32[]{:S(2)}, u32[]{:S(2)}) collective-permute-start(bf16[576,512]{1,0:T(8,128)(2,1)} %collective-permute-done.17.refs_4_), channel_id=1, source_target_pairs={{4,0},{0,4},{12,8},{8,12},{20,16},{16,20},{28,24},{24,28},{5,1},{1... | collective-permute-start | bytes 1769480 | tf_op jit(solution)/shard_map/ppermute | solution.py:79
  89.2 36.6 %collective-permute-start.1 = (bf16[576,512]{1,0:T(8,128)(2,1)S(1)}, bf16[576,512]{1,0:T(8,128)(2,1)S(1)}, u32[]{:S(2)}, u32[]{:S(2)}) collective-permute-start(bf16[576,512]{1,0:T(8,128)(2,1)S(1)} %copy-done.7), channel_id=1, source_target_pairs={{16,0},{20,4},{24,8},{28,12},{0,16},{4,20},{8,24},{12,28},{17,1},{... | collective-permute-start | bytes 1769480 | tf_op jit(solution)/shard_map/ppermute | solution.py:79
  91.5 37.3 %collective-permute-start.4 = (bf16[576,512]{1,0:T(8,128)(2,1)S(1)}, bf16[576,512]{1,0:T(8,128)(2,1)S(1)}, u32[]{:S(2)}, u32[]{:S(2)}) collective-permute-start(bf16[576,512]{1,0:T(8,128)(2,1)S(1)} %copy-done.12), channel_id=1, source_target_pairs={{8,0},{12,4},{0,8},{4,12},{24,16},{28,20},{16,24},{20,28},{9,1},{1... | collective-permute-start | bytes 1769480 | tf_op jit(solution)/shard_map/ppermute | solution.py:79
  93.8 36.5 %collective-permute-start.19 = (bf16[512,1152]{1,0:T(8,128)(2,1)S(1)}, bf16[512,1152]{1,0:T(8,128)(2,1)}, u32[]{:S(2)}, u32[]{:S(2)}) collective-permute-start(bf16[512,1152]{1,0:T(8,128)(2,1)S(1)} %constant_dynamic-slice_fusion.1), channel_id=1, source_target_pairs={{8,0},{12,4},{0,8},{4,12},{24,16},{28,20},{16,24},{20,28},{9,1},{1... | collective-permute-start | bytes 3538952 | tf_op jit(solution)/shard_map/ppermute | solution.py:79
  125.8 3.0 %copy-start.20 = (bf16[576,512]{1,0:T(8,128)(2,1)}, bf16[576,512]{1,0:T(8,128)(2,1)S(1)}, u32[]{:S(2)}) copy-start(bf16[576,512]{1,0:T(8,128)(2,1)S(1)} %collective-permute-done.1.refs_0_) | copy-start | bytes 1769476
  125.8 27.2 %collective-permute-start.7 = (bf16[576,1024]{1,0:T(8,128)(2,1)}, bf16[576,1024]{1,0:T(8,128)(2,1)}, u32[]{:S(2)}, u32[]{:S(2)}) collective-permute-start(bf16[576,1024]{1,0:T(8,128)(2,1)} %collective-permute-done.6.refs_7_), channel_id=1, source_target_pairs={{16,0},{20,4},{24,8},{28,12},{0,16},{4,20},{8,24},{12,28},{17,1},{... | collective-permute-start | bytes 3538952 | tf_op jit(solution)/shard_map/ppermute | solution.py:79
  127.3 27.5 %collective-permute-start.11 = (bf16[512,1152]{1,0:T(8,128)(2,1)}, bf16[512,1152]{1,0:T(8,128)(2,1)}, u32[]{:S(2)}, u32[]{:S(2)}) collective-permute-start(bf16[512,1152]{1,0:T(8,128)(2,1)} %collective-permute-done.10.refs_13_), channel_id=1, source_target_pairs={{8,0},{12,4},{0,8},{4,12},{24,16},{28,20},{16,24},{20,28},{9,1},{1... | collective-permute-start | bytes 3538952 | tf_op jit(solution)/shard_map/ppermute | solution.py:79
  128.8 1.5 copy-start.22
  128.8 26.1 %collective-permute-start.14 = (bf16[576,1024]{1,0:T(8,128)(2,1)}, bf16[576,1024]{1,0:T(8,128)(2,1)}, u32[]{:S(2)}, u32[]{:S(2)}) collective-permute-start(bf16[576,1024]{1,0:T(8,128)(2,1)} %collective-permute-done.13.refs_0_), channel_id=1, source_target_pairs={{4,0},{0,4},{12,8},{8,12},{20,16},{16,20},{28,24},{24,28},{5,1},{1... | collective-permute-start | bytes 3538952 | tf_op jit(solution)/shard_map/ppermute | solution.py:79
  128.8 1.1 copy-start.4
  129.9 25.6 %collective-permute-start.27 = (bf16[512,1152]{1,0:T(8,128)(2,1)}, bf16[512,1152]{1,0:T(8,128)(2,1)}, u32[]{:S(2)}, u32[]{:S(2)}) collective-permute-start(bf16[512,1152]{1,0:T(8,128)(2,1)} %collective-permute-done.10.refs_13_), channel_id=1, source_target_pairs={{4,0},{0,4},{12,8},{8,12},{20,16},{16,20},{28,24},{24,28},{5,1},{1... | collective-permute-start | bytes 3538952 | tf_op jit(solution)/shard_map/ppermute | solution.py:79
  130.3 44.8 %collective-permute-start.20 = (bf16[512,1152]{1,0:T(8,128)(2,1)}, bf16[512,1152]{1,0:T(8,128)(2,1)}, u32[]{:S(2)}, u32[]{:S(2)}) collective-permute-start(bf16[512,1152]{1,0:T(8,128)(2,1)} %collective-permute-done.19.refs_6_), channel_id=1, source_target_pairs={{4,0},{0,4},{12,8},{8,12},{20,16},{16,20},{28,24},{24,28},{5,1},{1... | collective-permute-start | bytes 3538952 | tf_op jit(solution)/shard_map/ppermute | solution.py:79
  153.0 27.9 %collective-permute-start.8 = (bf16[576,1024]{1,0:T(8,128)(2,1)}, bf16[576,1024]{1,0:T(8,128)(2,1)}, u32[]{:S(2)}, u32[]{:S(2)}) collective-permute-start(bf16[576,1024]{1,0:T(8,128)(2,1)} %collective-permute-done.7.refs_0_), channel_id=1, source_target_pairs={{4,0},{0,4},{12,8},{8,12},{20,16},{16,20},{28,24},{24,28},{5,1},{1... | collective-permute-start | bytes 3538952 | tf_op jit(solution)/shard_map/ppermute | solution.py:79
  154.8 26.0 %collective-permute-start.12 = (bf16[512,1152]{1,0:T(8,128)(2,1)}, bf16[512,1152]{1,0:T(8,128)(2,1)}, u32[]{:S(2)}, u32[]{:S(2)}) collective-permute-start(bf16[512,1152]{1,0:T(8,128)(2,1)} %collective-permute-done.11.refs_2_), channel_id=1, source_target_pairs={{4,0},{0,4},{12,8},{8,12},{20,16},{16,20},{28,24},{24,28},{5,1},{1... | collective-permute-start | bytes 3538952 | tf_op jit(solution)/shard_map/ppermute | solution.py:79
  154.9 30.3 %collective-permute-start.2 = (bf16[576,512]{1,0:T(8,128)(2,1)}, bf16[576,512]{1,0:T(8,128)(2,1)}, u32[]{:S(2)}, u32[]{:S(2)}) collective-permute-start(bf16[576,512]{1,0:T(8,128)(2,1)} %copy-done.20), channel_id=1, source_target_pairs={{4,0},{0,4},{12,8},{8,12},{20,16},{16,20},{28,24},{24,28},{5,1},{1... | collective-permute-start | bytes 1769480 | tf_op jit(solution)/shard_map/ppermute | solution.py:79
  155.5 29.7 %collective-permute-start.5 = (bf16[576,512]{1,0:T(8,128)(2,1)}, bf16[576,512]{1,0:T(8,128)(2,1)}, u32[]{:S(2)}, u32[]{:S(2)}) collective-permute-start(bf16[576,512]{1,0:T(8,128)(2,1)} %copy-done.22), channel_id=1, source_target_pairs={{4,0},{0,4},{12,8},{8,12},{20,16},{16,20},{28,24},{24,28},{5,1},{1... | collective-permute-start | bytes 1769480 | tf_op jit(solution)/shard_map/ppermute | solution.py:79
  158.5 1.3 copy-start.3
  159.7 1.3 copy-start.5
  161.0 1.1 copy-start.8
  162.1 1.1 copy-start.10
  163.1 1.1 copy-start.13
  164.2 1.1 copy-start.15
  165.3 1.1 copy-start.17
  166.3 1.1 copy-start.19
  167.4 7.8 %copy-start.25 = (bf16[576,512]{1,0:T(8,128)(2,1)S(1)}, bf16[576,512]{1,0:T(8,128)(2,1)}, u32[]{:S(2)}) copy-start(bf16[576,512]{1,0:T(8,128)(2,1)} %copy-done.24) | copy-start | bytes 1769476
  167.4 7.8 %copy-start.27 = (bf16[576,512]{1,0:T(8,128)(2,1)S(1)}, bf16[576,512]{1,0:T(8,128)(2,1)}, u32[]{:S(2)}) copy-start(bf16[576,512]{1,0:T(8,128)(2,1)} %copy-done.26) | copy-start | bytes 1769476
  180.9 4.3 %copy-start.21 = (bf16[576,512]{1,0:T(8,128)(2,1)S(1)}, bf16[576,512]{1,0:T(8,128)(2,1)}, u32[]{:S(2)}) copy-start(bf16[576,512]{1,0:T(8,128)(2,1)} %copy-done.20) | copy-start | bytes 1769476
  180.9 4.3 %copy-start.23 = (bf16[576,512]{1,0:T(8,128)(2,1)S(1)}, bf16[576,512]{1,0:T(8,128)(2,1)}, u32[]{:S(2)}) copy-start(bf16[576,512]{1,0:T(8,128)(2,1)} %copy-done.22) | copy-start | bytes 1769476
  185.2 3.1 %copy-start.1 = (bf16[1024,64]{0,1:T(8,128)(2,1)S(1)}, bf16[1024,64]{0,1:T(8,128)(2,1)}, u32[]{:S(2)}) copy-start(bf16[1024,64]{0,1:T(8,128)(2,1)} %param.24) | copy-start | bytes 393220
  (7 other events, 6.0 us)
where the time goes:
time: 189 us; the launch traced here: 188 us
  waiting for transfers between devices  101 us (53%)
  starting transfers between devices  27.3 us (14%)
  local copies, waits for them, and re-layouts  24.4 us (13%)
  Pallas kernels  20.8 us (11%)
  other arithmetic  7.29 us (4%)
  matrix products  6.54 us (3%)
    ppermute x32, waiting for transfers between devices, shift(): return lax.ppermute(value, 'zero', pairs)  101 us
    ppermute x32, starting transfers between devices, shift(): return lax.ppermute(value, 'zero', pairs)  21.2 us
    pallas_call x4, Pallas kernels, place(): pl.pallas_call(body, out_shape=[jax.ShapeDtypeStruct(shape, jnp.bfloat16)...  20.8 us
    unnamed x72, local copies, waits for them, and re-layouts  16.1 us
    dot_general x4, matrix products, merged(): update = jnp.dot(low, high, preferred_element_type=jnp.float32)  6.54 us
    ppermute x3, starting transfers between devices, gather_norm(): around.append(lax.ppermute(norm, 'width', pairs))  6.09 us
    select_n x1, other arithmetic, on_device(): jnp.where(core == 0, jnp.concatenate([mixed, other_mixed], axis=1), jnp.c...  5.1 us
    convert_element_type x2, local copies, waits for them, and re-layouts, merged(): return (train.astype(jnp.float32) + mix_rate * update).astype(jnp.bfloat16)  4.22 us
  transfers between devices with their start and end apart: 35, of which 10 were waited for; matrix products, arithmetic and copies ran while one was open for 11% of the time, Pallas kernels for 9%

commit v1 on v0

--- a/solution.py
+++ b/solution.py
@@ -102,7 +102,8 @@
     spots = [(dy, dx) for dy in range(side_y) for dx in range(side_x)]
     groups = [
         [(output, (0, 0)) for output in range(4)]
-        + [(output, spot) for output in (0, 1) for spot in spots if spot[0] == 0 and spot[1] > 0]
+        + [(1, spot) for spot in spots if spot != (0, 0) and 0 in spot]
+        + [(0, spot) for spot in spots if spot[0] == 0 and spot[1] > 0]
         + [(output, spot) for output in (2, 3) for spot in spots if spot[1] == 0 and spot[0] > 0],
     ]
     rest = [(output, spot) for output in range(4) for spot in spots if (output, spot) not in groups[0]]
@@ -130,9 +131,9 @@
     ):
         norm = (norm_train + norm_step).astype(jnp.bfloat16)
         key = merged(train_key, low_key, high_key)
-        mixed = merged(train_mixed, low_mixed, high_mixed)
         value = merged(train_value, low_value, high_value)
         query = merged(train_query, low_query, high_query)
+        mixed = merged(train_mixed, low_mixed, high_mixed)
         rows, columns = query.shape[0], mixed.shape[1]
         aligned = rows % 16 == 0 and (cores * columns) % 128 == 0
         aligned = aligned and mixed.shape[0] % (16 * cores) == 0
@@ -214,11 +215,14 @@
             (mixed.shape[0], columns * zero),
         ]
         held_of = (queries, keys, values, mixeds)
+        serving_norm = gather_norm(norm, y, x, core)
         outputs = [None] * 4
-        for group in groups:
+        for step, group in enumerate(groups):
+            if step == 2:
+                offsets, serving_norm = lax.optimization_barrier((offsets, serving_norm))
             moves = [move for output, spot in group for move in moves_of(held_of[output], output, spot)]
             outputs = place(outputs, moves, offsets, shapes)
-        return (*outputs, gather_norm(norm, y, x, core))
+        return (*outputs, serving_norm)
 
     return jax.shard_map(
         on_device,

time: 189 us -> 205 us (1.085)
  waiting for transfers between devices: 101 us -> 115 us
  starting transfers between devices: 27.3 us -> 30.6 us
    ppermute x32, waiting for transfers between devices: 101 us -> 115 us  [shift(): return lax.ppermute(value, 'zero', pairs)]
    unnamed x72 -> x60, local copies, waits for them, and re-layouts: 16.1 us -> 12.2 us
    ppermute x32, starting transfers between devices: 21.2 us -> 24.5 us  [shift(): return lax.ppermute(value, 'zero', pairs)]
    another operation x4, local copies, waits for them, and re-layouts: 0.02 us -> 2.55 us  [gather_norm(): gathered = jnp.roll(jnp.stack(around), lax.axis_index('width'), axis=0)]
where the time goes in v1:
time: 205 us
  waiting for transfers between devices  115 us (56%)
  starting transfers between devices  30.6 us (15%)
  local copies, waits for them, and re-layouts  23.7 us (12%)
  Pallas kernels  21.4 us (10%)
  other arithmetic  7.31 us (4%)
  matrix products  5.33 us (3%)
    ppermute x32, waiting for transfers between devices, shift(): return lax.ppermute(value, 'zero', pairs)  115 us
    ppermute x32, starting transfers between devices, shift(): return lax.ppermute(value, 'zero', pairs)  24.5 us
    pallas_call x4, Pallas kernels, place(): pl.pallas_call(body, out_shape=[jax.ShapeDtypeStruct(shape, jnp.bfloat16)...  21.4 us
    unnamed x60, local copies, waits for them, and re-layouts  12.2 us
    ppermute x3, starting transfers between devices, gather_norm(): around.append(lax.ppermute(norm, 'width', pairs))  6.09 us
    dot_general x4, matrix products, merged(): update = jnp.dot(low, high, preferred_element_type=jnp.float32)  5.33 us
    select_n x1, other arithmetic, on_device(): jnp.where(core == 0, jnp.concatenate([mixed, other_mixed], axis=1), jnp.c...  5.09 us
    convert_element_type x2, local copies, waits for them, and re-layouts, merged(): return (train.astype(jnp.float32) + mix_rate * update).astype(jnp.bfloat16)  4.22 us
  transfers between devices with their start and end apart: 35, of which 10 were waited for; matrix products, arithmetic and copies ran while one was open for 11% of the time, Pallas kernels for 9%

profile of v1, /device:TPU:0, one launch (start us, length us, event | category | flops | bytes accessed | tf_op | source)
XLA Modules:
  0.0 204.8 jit_solution(18364880907058782709)
XLA Ops:
  0.7 0.7 add_convert_fusion.2
  1.4 5.1 %collective-permute-start = (bf16[144]{0:T(256)(128)(2,1)S(1)}, bf16[144]{0:T(256)(128)(2,1)S(1)}, u32[]{:S(2)}, u32[]{:S(2)}) collective-permute-start(bf16[144]{0:T(256)(128)(2,1)S(1)} %add_convert_fusion.2), channel_id=1, source_target_pairs={{1,0},{2,1},{3,2},{0,3},{5,4},{6,5},{7,6},{4,7},{9,8},{10,9},{11,1... | collective-permute-start | bytes 872 | tf_op jit(solution)/shard_map/ppermute | solution.py:85
  6.5 1.0 collective-permute-start.2
  7.5 2.8 %copy.39 = f32[1024,576]{1,0:T(8,128)} copy(bf16[1024,576]{0,1:T(8,128)(2,1)} %param.23) | data formatting | bytes 3538944 | tf_op jit(solution)/shard_map/convert_element_type | solution.py:16
  10.3 2.3 %add_convert_fusion = bf16[1024,576]{1,0:T(8,128)(2,1)S(1)} fusion(f32[1024,576]{1,0:T(8,128)} %copy.39, bf16[1024,64]{0,1:T(8,128)(2,1)S(1)} %copy-done, bf16[64,576]{1,0:T(8,128)(2,1)S(1)} %copy-done.24), kind=kOutput, calls=%fused_computation | convolution fusion | flops 77266944 | bytes 3743744 | tf_op jit(solution)/shard_map/dot_general | solution.py:15
  12.7 1.4 copy.40
  14.5 1.6 collective-permute-start.7
  16.1 1.4 add_convert_fusion.1.refs_0_
  17.5 1.2 fusion.2.refs_4_
  18.8 0.5 copy-done.29
  19.3 0.5 collective-permute-start.13
  19.8 0.7 stack.96
  20.5 0.5 copy-done.28
  21.0 1.5 collective-permute-start.10
  22.5 0.7 stack.97
  23.2 1.2 stack.98
  24.4 0.8 concatenate.25
  25.3 1.1 collective-permute-done.3
  26.5 1.6 collective-permute-start.4
  28.0 27.6 %collective-permute-done.4 = bf16[2,4,144]{2,1,0:T(4,128)(2,1)S(1)} collective-permute-done((bf16[2,4,144]{2,1,0:T(4,128)(2,1)S(1)}, bf16[2,4,144]{2,1,0:T(4,128)(2,1)S(1)}, u32[]{:S(2)}, u32[]{:S(2)}) %collective-permute-start.4) | collective-permute-done | bytes 2336 | tf_op jit(solution)/shard_map/ppermute | solution.py:79
  55.7 1.5 collective-permute-start.5
  57.2 2.1 %collective-permute-done.5 = bf16[2,4,144]{2,1,0:T(4,128)(2,1)S(1)} collective-permute-done((bf16[2,4,144]{2,1,0:T(4,128)(2,1)S(1)}, bf16[2,4,144]{2,1,0:T(4,128)(2,1)S(1)}, u32[]{:S(2)}, u32[]{:S(2)}) %collective-permute-start.5) | collective-permute-done | bytes 2336 | tf_op jit(solution)/shard_map/ppermute | solution.py:79
  59.3 2.4 %collective-permute-start.6 = (bf16[2,4,144]{2,1,0:T(4,128)(2,1)S(1)}, bf16[2,4,144]{2,1,0:T(4,128)(2,1)S(1)}, u32[]{:S(2)}, u32[]{:S(2)}) collective-permute-start(bf16[2,4,144]{2,1,0:T(4,128)(2,1)S(1)} %fusion.8), channel_id=1, source_target_pairs={{24,0},{28,4},{16,8},{20,12},{8,16},{12,20},{0,24},{4,28},{25,1},{... | collective-permute-start | bytes 6920 | tf_op jit(solution)/shard_map/ppermute | solution.py:79
  61.7 2.2 %collective-permute-done.6 = bf16[2,4,144]{2,1,0:T(4,128)(2,1)S(1)} collective-permute-done((bf16[2,4,144]{2,1,0:T(4,128)(2,1)S(1)}, bf16[2,4,144]{2,1,0:T(4,128)(2,1)S(1)}, u32[]{:S(2)}, u32[]{:S(2)}) %collective-permute-start.6) | collective-permute-done | bytes 2336 | tf_op jit(solution)/shard_map/ppermute | solution.py:79
  63.9 1.5 collective-permute-start.30
  65.4 0.5 collective-permute-start.28
  65.9 1.6 collective-permute-start.22
  67.5 2.4 %copy.41 = bf16[1024,576]{1,0:T(8,128)(2,1)} copy(bf16[1024,576]{0,1:T(8,128)(2,1)} %collective-permute-done.16) | data formatting | bytes 2359296 | tf_op jit(solution)/shard_map/ppermute | solution.py:79
  69.9 6.6 %collective-permute-done.30.refs_9_ = bf16[576,512]{1,0:T(8,128)(2,1)} collective-permute-done((bf16[576,512]{1,0:T(8,128)(2,1)S(1)}, bf16[576,512]{1,0:T(8,128)(2,1)}, u32[]{:S(2)}, u32[]{:S(2)}) %collective-permute-start.30) | collective-permute-done | bytes 589856 | tf_op jit(solution)/shard_map/ppermute | solution.py:79
  76.5 0.5 collective-permute-start.29
  77.0 5.1 %maximum_select_fusion.refs_6_ = bf16[1024,1152]{1,0:T(8,128)(2,1)S(1)} fusion(bf16[1024,576]{1,0:T(8,128)(2,1)} %copy.41, bf16[1024,576]{1,0:T(8,128)(2,1)} %copy-done.19, pred[]{:T(512)S(6)} %eq.23), kind=kLoop, calls=%fused_computation.1 | loop fusion | flops 10616832 | bytes 4718593 | tf_op jit(solution)/shard_map/jit(_where)/select_n | solution.py:155
  82.1 1.6 collective-permute-start.20
  83.7 0.5 collective-permute-start.31
  84.3 0.8 copy-done.6
  85.2 0.5 collective-permute-start.17
  85.9 0.8 copy-done.8
  86.9 0.8 copy-done.10
  87.7 0.4 collective-permute-start.23
  88.1 1.0 copy-done.2
  89.1 1.5 collective-permute-start.11
  90.6 20.6 %collective-permute-done.20.refs_0_ = bf16[576,1024]{1,0:T(8,128)(2,1)} collective-permute-done((bf16[576,1024]{1,0:T(8,128)(2,1)S(1)}, bf16[576,1024]{1,0:T(8,128)(2,1)}, u32[]{:S(2)}, u32[]{:S(2)}) %collective-permute-start.20) | collective-permute-done | bytes 1179680 | tf_op jit(solution)/shard_map/ppermute | solution.py:79
  111.1 1.5 collective-permute-start.8
  112.7 0.8 copy-done.16
  113.5 1.5 collective-permute-start.24
  115.0 0.5 collective-permute-start.14
  115.5 20.9 %collective-permute-done.17.refs_15_ = bf16[512,1152]{1,0:T(8,128)(2,1)} collective-permute-done((bf16[512,1152]{1,0:T(8,128)(2,1)S(1)}, bf16[512,1152]{1,0:T(8,128)(2,1)}, u32[]{:S(2)}, u32[]{:S(2)}) %collective-permute-start.17) | collective-permute-done | bytes 1179680 | tf_op jit(solution)/shard_map/ppermute | solution.py:79
  136.4 1.5 collective-permute-start.18
  137.9 11.1 %collective-permute-done.8.refs_0_ = bf16[576,512]{1,0:T(8,128)(2,1)S(1)} collective-permute-done((bf16[576,512]{1,0:T(8,128)(2,1)}, bf16[576,512]{1,0:T(8,128)(2,1)S(1)}, u32[]{:S(2)}, u32[]{:S(2)}) %collective-permute-start.8) | collective-permute-done | bytes 589856 | tf_op jit(solution)/shard_map/ppermute | solution.py:79
  149.0 1.1 copy-done.4
  150.0 0.5 collective-permute-start.34
  150.5 22.8 %collective-permute-done.14.refs_0_ = bf16[576,1024]{1,0:T(8,128)(2,1)} collective-permute-done((bf16[576,1024]{1,0:T(8,128)(2,1)S(1)}, bf16[576,1024]{1,0:T(8,128)(2,1)}, u32[]{:S(2)}, u32[]{:S(2)}) %collective-permute-start.14) | collective-permute-done | bytes 1179680 | tf_op jit(solution)/shard_map/ppermute | solution.py:79
  173.4 0.6 collective-permute-start.19
  174.7 1.3 pad_maximum_fusion
  176.0 0.8 reshape.16
  176.9 0.6 reshape.17
  177.6 1.3 copy-done.3
  178.8 1.3 copy-done.5
  180.1 1.1 copy-done.7
  181.2 1.1 copy-done.9
  182.2 1.1 copy-done.11
  183.3 9.0 %shard_map.173 = (bf16[4608,1024]{1,0:T(8,128)(2,1)}, bf16[4608,512]{1,0:T(8,128)(2,1)}, bf16[4608,512]{1,0:T(8,128)(2,1)}, bf16[1024,4608]{1,0:T(8,128)(2,1)}) custom-call(s32[15]{0:T(128)S(1)} %stack.94.offsets_ref, bf16[576,1024]{1,0:T(8,128)(2,1)S(1)} %add_convert_fusion.1.refs_0_, bf16[576,1024]{1,0:T(8,128)(2,1)S(1)} %copy-done.3, ...), custom_call_target="tpu_custom_call" | custom-call | tf_op jit(solution)/shard_map/pallas_call | solution.py:50
  192.3 5.0 %shard_map.174 = (bf16[4608,1024]{1,0:T(8,128)(2,1)}, bf16[4608,512]{1,0:T(8,128)(2,1)}, bf16[4608,512]{1,0:T(8,128)(2,1)}, bf16[1024,4608]{1,0:T(8,128)(2,1)}) custom-call(s32[15]{0:T(128)S(1)} %stack.94.offsets_ref, bf16[576,1024]{1,0:T(8,128)(2,1)} %collective-permute-done.20.refs_0_, ...), custom_call_target="tpu_custom_call", output_to_operand_aliasing={{0}: (7, {}), {1}: (8, {}), {2}: (9, {}), {3}: (10, {})} | custom-call | tf_op jit(solution)/shard_map/pallas_call | solution.py:50
  197.3 4.3 %shard_map.175 = (bf16[4608,1024]{1,0:T(8,128)(2,1)}, bf16[4608,512]{1,0:T(8,128)(2,1)}, bf16[4608,512]{1,0:T(8,128)(2,1)}, bf16[1024,4608]{1,0:T(8,128)(2,1)}) custom-call(s32[15]{0:T(128)S(1)} %stack.94.offsets_ref, bf16[576,1024]{1,0:T(8,128)(2,1)} %collective-permute-done.14.refs_0_, ...), custom_call_target="tpu_custom_call", output_to_operand_aliasing={{0}: (5, {}), {1}: (6, {}), {2}: (7, {}), {3}: (8, {})} | custom-call | tf_op jit(solution)/shard_map/pallas_call | solution.py:50
  201.7 3.1 %shard_map.176 = (bf16[4608,1024]{1,0:T(8,128)(2,1)}, bf16[4608,512]{1,0:T(8,128)(2,1)}, bf16[4608,512]{1,0:T(8,128)(2,1)}, bf16[1024,4608]{1,0:T(8,128)(2,1)}) custom-call(s32[15]{0:T(128)S(1)} %stack.94.offsets_ref, bf16[576,512]{1,0:T(8,128)(2,1)S(1)} %copy-done.15, ...), custom_call_target="tpu_custom_call", output_to_operand_aliasing={{0}: (5, {}), {1}: (6, {}), {2}: (7, {}), {3}: (8, {})} | custom-call | tf_op jit(solution)/shard_map/pallas_call | solution.py:50
  (95 shorter events, 2.0 us)
Async XLA Ops:
  0.6 9.7 %copy-start = (bf16[1024,64]{0,1:T(8,128)(2,1)S(1)}, bf16[1024,64]{0,1:T(8,128)(2,1)}, u32[]{:S(2)}) copy-start(bf16[1024,64]{0,1:T(8,128)(2,1)} %param.24) | copy-start | bytes 393220
  0.6 9.6 %copy-start.24 = (bf16[64,576]{1,0:T(8,128)(2,1)S(1)}, bf16[64,576]{1,0:T(8,128)(2,1)}, u32[]{:S(2)}) copy-start(bf16[64,576]{1,0:T(8,128)(2,1)} %param.25) | copy-start | bytes 221188
  1.4 17.4 %collective-permute-start = (bf16[144]{0:T(256)(128)(2,1)S(1)}, bf16[144]{0:T(256)(128)(2,1)S(1)}, u32[]{:S(2)}, u32[]{:S(2)}) collective-permute-start(bf16[144]{0:T(256)(128)(2,1)S(1)} %add_convert_fusion.2), channel_id=1, source_target_pairs={{1,0},{2,1},{3,2},{0,3},{5,4},{6,5},{7,6},{4,7},{9,8},{10,9},{11,1... | collective-permute-start | bytes 872 | tf_op jit(solution)/shard_map/ppermute | solution.py:85
  6.5 14.0 %collective-permute-start.1 = (bf16[144]{0:T(256)(128)(2,1)S(1)}, bf16[144]{0:T(256)(128)(2,1)S(1)}, u32[]{:S(2)}, u32[]{:S(2)}) collective-permute-start(bf16[144]{0:T(256)(128)(2,1)S(1)} %add_convert_fusion.2), channel_id=1, source_target_pairs={{2,0},{3,1},{0,2},{1,3},{6,4},{7,5},{4,6},{5,7},{10,8},{11,9},{8,1... | collective-permute-start | bytes 872 | tf_op jit(solution)/shard_map/ppermute | solution.py:85
  6.5 16.7 %collective-permute-start.2 = (bf16[144]{0:T(256)(128)(2,1)S(1)}, bf16[144]{0:T(256)(128)(2,1)}, u32[]{:S(2)}, u32[]{:S(2)}) collective-permute-start(bf16[144]{0:T(256)(128)(2,1)S(1)} %add_convert_fusion.2), channel_id=1, source_target_pairs={{3,0},{0,1},{1,2},{2,3},{7,4},{4,5},{5,6},{6,7},{11,8},{8,9},{9,10... | collective-permute-start | bytes 872 | tf_op jit(solution)/shard_map/ppermute | solution.py:85
  10.3 3.8 %copy-start.21 = (bf16[576,512]{1,0:T(8,128)(2,1)S(1)}, bf16[576,512]{1,0:T(8,128)(2,1)}, u32[]{:S(2)}) copy-start(bf16[576,512]{1,0:T(8,128)(2,1)} %param.17) | copy-start | bytes 1769476
  10.3 3.8 %copy-start.23 = (bf16[576,64]{0,1:T(8,128)(2,1)S(1)}, bf16[576,64]{0,1:T(8,128)(2,1)}, u32[]{:S(2)}) copy-start(bf16[576,64]{0,1:T(8,128)(2,1)} %param.18) | copy-start | bytes 221188
  10.3 3.8 %copy-start.25 = (bf16[64,512]{1,0:T(8,128)(2,1)S(1)}, bf16[64,512]{1,0:T(8,128)(2,1)}, u32[]{:S(2)}) copy-start(bf16[64,512]{1,0:T(8,128)(2,1)} %param.19) | copy-start | bytes 196612
  12.7 1.4 copy-start.19
  12.7 3.4 %copy-start.20 = (bf16[576,1024]{1,0:T(8,128)(2,1)S(1)}, bf16[576,1024]{1,0:T(8,128)(2,1)}, u32[]{:S(2)}) copy-start(bf16[576,1024]{1,0:T(8,128)(2,1)} %param.14) | copy-start | bytes 3538948
  14.1 51.8 %collective-permute-start.16 = (bf16[1024,576]{0,1:T(8,128)(2,1)}, bf16[1024,576]{0,1:T(8,128)(2,1)}, u32[]{:S(2)}, u32[]{:S(2)}) collective-permute-start(bf16[1024,576]{0,1:T(8,128)(2,1)} %copy.40), channel_id=1, source_target_pairs={{4,0},{0,4},{12,8},{8,12},{20,16},{16,20},{28,24},{24,28},{5,1},{1... | collective-permute-start | bytes 3538952 | tf_op jit(solution)/shard_map/ppermute | solution.py:79
  14.5 3.0 %copy-start.22 = (bf16[576,512]{1,0:T(8,128)(2,1)S(1)}, bf16[576,512]{1,0:T(8,128)(2,1)}, u32[]{:S(2)}) copy-start(bf16[576,512]{1,0:T(8,128)(2,1)} %param.20) | copy-start | bytes 1769476
  14.5 50.9 %collective-permute-start.7 = (bf16[576,512]{1,0:T(8,128)(2,1)S(1)}, bf16[576,512]{1,0:T(8,128)(2,1)}, u32[]{:S(2)}, u32[]{:S(2)}) collective-permute-start(bf16[576,512]{1,0:T(8,128)(2,1)S(1)} %fusion.3.refs_2_), channel_id=1, source_target_pairs={{8,0},{12,4},{0,8},{4,12},{24,16},{28,20},{16,24},{20,28},{9,1},{1... | collective-permute-start | bytes 1769480 | tf_op jit(solution)/shard_map/ppermute | solution.py:79
  18.8 0.5 copy-start.29
  19.3 64.4 %collective-permute-start.13 = (bf16[576,1024]{1,0:T(8,128)(2,1)S(1)}, bf16[576,1024]{1,0:T(8,128)(2,1)S(1)}, u32[]{:S(2)}, u32[]{:S(2)}) collective-permute-start(bf16[576,1024]{1,0:T(8,128)(2,1)S(1)} %add_convert_fusion.1.refs_0_), channel_id=1, source_target_pairs={{8,0},{12,4},{0,8},{4,12},{24,16},{28,20},{16,24},{20,28},{9,1},{1... | collective-permute-start | bytes 3538952 | tf_op jit(solution)/shard_map/ppermute | solution.py:79
  21.0 44.4 %collective-permute-start.10 = (bf16[576,512]{1,0:T(8,128)(2,1)S(1)}, bf16[576,512]{1,0:T(8,128)(2,1)}, u32[]{:S(2)}, u32[]{:S(2)}) collective-permute-start(bf16[576,512]{1,0:T(8,128)(2,1)S(1)} %fusion.2.refs_4_), channel_id=1, source_target_pairs={{16,0},{20,4},{24,8},{28,12},{0,16},{4,20},{8,24},{12,28},{17,1},{... | collective-permute-start | bytes 1769480 | tf_op jit(solution)/shard_map/ppermute | solution.py:79
  25.2 1.2 collective-permute-start.3
  26.5 29.2 %collective-permute-start.4 = (bf16[2,4,144]{2,1,0:T(4,128)(2,1)S(1)}, bf16[2,4,144]{2,1,0:T(4,128)(2,1)S(1)}, u32[]{:S(2)}, u32[]{:S(2)}) collective-permute-start(bf16[2,4,144]{2,1,0:T(4,128)(2,1)S(1)} %fusion.8), channel_id=1, source_target_pairs={{8,0},{12,4},{0,8},{4,12},{24,16},{28,20},{16,24},{20,28},{9,1},{1... | collective-permute-start | bytes 6920 | tf_op jit(solution)/shard_map/ppermute | solution.py:79
  55.7 3.6 %collective-permute-start.5 = (bf16[2,4,144]{2,1,0:T(4,128)(2,1)S(1)}, bf16[2,4,144]{2,1,0:T(4,128)(2,1)S(1)}, u32[]{:S(2)}, u32[]{:S(2)}) collective-permute-start(bf16[2,4,144]{2,1,0:T(4,128)(2,1)S(1)} %fusion.8), channel_id=1, source_target_pairs={{16,0},{20,4},{24,8},{28,12},{0,16},{4,20},{8,24},{12,28},{17,1},{... | collective-permute-start | bytes 6920 | tf_op jit(solution)/shard_map/ppermute | solution.py:79
  59.3 6.7 %copy-start.26 = (bf16[2,4,144]{2,1,0:T(4,128)(2,1)}, bf16[2,4,144]{2,1,0:T(4,128)(2,1)S(1)}, u32[]{:S(2)}) copy-start(bf16[2,4,144]{2,1,0:T(4,128)(2,1)S(1)} %collective-permute-done.5) | copy-start | bytes 6916
  59.3 4.6 %collective-permute-start.6 = (bf16[2,4,144]{2,1,0:T(4,128)(2,1)S(1)}, bf16[2,4,144]{2,1,0:T(4,128)(2,1)S(1)}, u32[]{:S(2)}, u32[]{:S(2)}) collective-permute-start(bf16[2,4,144]{2,1,0:T(4,128)(2,1)S(1)} %fusion.8), channel_id=1, source_target_pairs={{24,0},{28,4},{16,8},{20,12},{8,16},{12,20},{0,24},{4,28},{25,1},{... | collective-permute-start | bytes 6920 | tf_op jit(solution)/shard_map/ppermute | solution.py:79
  63.9 2.0 copy-start.27
  63.9 12.6 %collective-permute-start.30 = (bf16[576,512]{1,0:T(8,128)(2,1)S(1)}, bf16[576,512]{1,0:T(8,128)(2,1)}, u32[]{:S(2)}, u32[]{:S(2)}) collective-permute-start(bf16[576,512]{1,0:T(8,128)(2,1)S(1)} %fusion.3.refs_2_), channel_id=1, source_target_pairs={{16,0},{20,4},{24,8},{28,12},{0,16},{4,20},{8,24},{12,28},{17,1},{... | collective-permute-start | bytes 1769480 | tf_op jit(solution)/shard_map/ppermute | solution.py:79
  65.4 11.1 %collective-permute-start.27 = (bf16[576,512]{1,0:T(8,128)(2,1)S(1)}, bf16[576,512]{1,0:T(8,128)(2,1)}, u32[]{:S(2)}, u32[]{:S(2)}) collective-permute-start(bf16[576,512]{1,0:T(8,128)(2,1)S(1)} %fusion.3.refs_2_), channel_id=1, source_target_pairs={{4,0},{0,4},{12,8},{8,12},{20,16},{16,20},{28,24},{24,28},{5,1},{1... | collective-permute-start | bytes 1769480 | tf_op jit(solution)/shard_map/ppermute | solution.py:79
  65.4 16.7 %collective-permute-start.28 = (bf16[576,512]{1,0:T(8,128)(2,1)S(1)}, bf16[576,512]{1,0:T(8,128)(2,1)}, u32[]{:S(2)}, u32[]{:S(2)}) collective-permute-start(bf16[576,512]{1,0:T(8,128)(2,1)S(1)} %fusion.2.refs_4_), channel_id=1, source_target_pairs={{4,0},{0,4},{12,8},{8,12},{20,16},{16,20},{28,24},{24,28},{5,1},{1... | collective-permute-start | bytes 1769480 | tf_op jit(solution)/shard_map/ppermute | solution.py:79
  65.9 17.8 %collective-permute-start.22 = (bf16[576,512]{1,0:T(8,128)(2,1)S(1)}, bf16[576,512]{1,0:T(8,128)(2,1)}, u32[]{:S(2)}, u32[]{:S(2)}) collective-permute-start(bf16[576,512]{1,0:T(8,128)(2,1)S(1)} %fusion.2.refs_4_), channel_id=1, source_target_pairs={{8,0},{12,4},{0,8},{4,12},{24,16},{28,20},{16,24},{20,28},{9,1},{1... | collective-permute-start | bytes 1769480 | tf_op jit(solution)/shard_map/ppermute | solution.py:79
  76.5 11.6 %collective-permute-start.26 = (bf16[576,1024]{1,0:T(8,128)(2,1)S(1)}, bf16[576,1024]{1,0:T(8,128)(2,1)S(1)}, u32[]{:S(2)}, u32[]{:S(2)}) collective-permute-start(bf16[576,1024]{1,0:T(8,128)(2,1)S(1)} %add_convert_fusion.1.refs_0_), channel_id=1, source_target_pairs={{4,0},{0,4},{12,8},{8,12},{20,16},{16,20},{28,24},{24,28},{5,1},{1... | collective-permute-start | bytes 3538952 | tf_op jit(solution)/shard_map/ppermute | solution.py:79
  76.5 7.8 %collective-permute-start.29 = (bf16[576,512]{1,0:T(8,128)(2,1)}, bf16[576,512]{1,0:T(8,128)(2,1)S(1)}, u32[]{:S(2)}, u32[]{:S(2)}) collective-permute-start(bf16[576,512]{1,0:T(8,128)(2,1)} %collective-permute-done.7.refs_7_), channel_id=1, source_target_pairs={{4,0},{0,4},{12,8},{8,12},{20,16},{16,20},{28,24},{24,28},{5,1},{1... | collective-permute-start | bytes 1769480 | tf_op jit(solution)/shard_map/ppermute | solution.py:79
  82.1 91.3 %copy-start.18 = (bf16[1024,1152]{1,0:T(8,128)(2,1)}, bf16[1024,1152]{1,0:T(8,128)(2,1)S(1)}, u32[]{:S(2)}) copy-start(bf16[1024,1152]{1,0:T(8,128)(2,1)S(1)} %maximum_select_fusion.refs_6_) | copy-start | bytes 7077892
  82.1 29.0 %collective-permute-start.20 = (bf16[576,1024]{1,0:T(8,128)(2,1)S(1)}, bf16[576,1024]{1,0:T(8,128)(2,1)}, u32[]{:S(2)}, u32[]{:S(2)}) collective-permute-start(bf16[576,1024]{1,0:T(8,128)(2,1)S(1)} %add_convert_fusion.1.refs_0_), channel_id=1, source_target_pairs={{16,0},{20,4},{24,8},{28,12},{0,16},{4,20},{8,24},{12,28},{17,1},{... | collective-permute-start | bytes 3538952 | tf_op jit(solution)/shard_map/ppermute | solution.py:79
  83.7 2.2 %collective-permute-start.33 = (bf16[576,512]{1,0:T(8,128)(2,1)}, bf16[576,512]{1,0:T(8,128)(2,1)S(1)}, u32[]{:S(2)}, u32[]{:S(2)}) collective-permute-start(bf16[576,512]{1,0:T(8,128)(2,1)} %collective-permute-done.10.refs_13_), channel_id=1, source_target_pairs={{4,0},{0,4},{12,8},{8,12},{20,16},{16,20},{28,24},{24,28},{5,1},{1... | collective-permute-start | bytes 1769480 | tf_op jit(solution)/shard_map/ppermute | solution.py:79
  83.7 3.2 %collective-permute-start.31 = (bf16[576,512]{1,0:T(8,128)(2,1)}, bf16[576,512]{1,0:T(8,128)(2,1)S(1)}, u32[]{:S(2)}, u32[]{:S(2)}) collective-permute-start(bf16[576,512]{1,0:T(8,128)(2,1)} %collective-permute-done.30.refs_9_), channel_id=1, source_target_pairs={{4,0},{0,4},{12,8},{8,12},{20,16},{16,20},{28,24},{24,28},{5,1},{1... | collective-permute-start | bytes 1769480 | tf_op jit(solution)/shard_map/ppermute | solution.py:79
  84.3 0.8 copy-start.6
  85.2 51.3 %collective-permute-start.17 = (bf16[512,1152]{1,0:T(8,128)(2,1)S(1)}, bf16[512,1152]{1,0:T(8,128)(2,1)}, u32[]{:S(2)}, u32[]{:S(2)}) collective-permute-start(bf16[512,1152]{1,0:T(8,128)(2,1)S(1)} %constant_dynamic-slice_fusion), channel_id=1, source_target_pairs={{16,0},{20,4},{24,8},{28,12},{0,16},{4,20},{8,24},{12,28},{17,1},{... | collective-permute-start | bytes 3538952 | tf_op jit(solution)/shard_map/ppermute | solution.py:79
  85.9 0.8 copy-start.8
  86.7 62.2 %collective-permute-start.32 = (bf16[576,1024]{1,0:T(8,128)(2,1)S(1)}, bf16[576,1024]{1,0:T(8,128)(2,1)S(1)}, u32[]{:S(2)}, u32[]{:S(2)}) collective-permute-start(bf16[576,1024]{1,0:T(8,128)(2,1)S(1)} %collective-permute-done.13.refs_11_), channel_id=1, source_target_pairs={{4,0},{0,4},{12,8},{8,12},{20,16},{16,20},{28,24},{24,28},{5,1},{1... | collective-permute-start | bytes 3538952 | tf_op jit(solution)/shard_map/ppermute | solution.py:79
  86.9 0.8 copy-start.10
  87.7 25.0 %collective-permute-start.23 = (bf16[576,512]{1,0:T(8,128)(2,1)}, bf16[576,512]{1,0:T(8,128)(2,1)S(1)}, u32[]{:S(2)}, u32[]{:S(2)}) collective-permute-start(bf16[576,512]{1,0:T(8,128)(2,1)} %collective-permute-done.22.refs_2_), channel_id=1, source_target_pairs={{4,0},{0,4},{12,8},{8,12},{20,16},{16,20},{28,24},{24,28},{5,1},{1... | collective-permute-start | bytes 1769480 | tf_op jit(solution)/shard_map/ppermute | solution.py:79
  88.1 1.0 copy-start.2
  89.1 25.9 %collective-permute-start.11 = (bf16[576,512]{1,0:T(8,128)(2,1)}, bf16[576,512]{1,0:T(8,128)(2,1)S(1)}, u32[]{:S(2)}, u32[]{:S(2)}) collective-permute-start(bf16[576,512]{1,0:T(8,128)(2,1)} %collective-permute-done.10.refs_13_), channel_id=1, source_target_pairs={{8,0},{12,4},{0,8},{4,12},{24,16},{28,20},{16,24},{20,28},{9,1},{1... | collective-permute-start | bytes 1769480 | tf_op jit(solution)/shard_map/ppermute | solution.py:79
  111.1 37.8 %collective-permute-start.8 = (bf16[576,512]{1,0:T(8,128)(2,1)}, bf16[576,512]{1,0:T(8,128)(2,1)S(1)}, u32[]{:S(2)}, u32[]{:S(2)}) collective-permute-start(bf16[576,512]{1,0:T(8,128)(2,1)} %collective-permute-done.7.refs_7_), channel_id=1, source_target_pairs={{16,0},{20,4},{24,8},{28,12},{0,16},{4,20},{8,24},{12,28},{17,1},{... | collective-permute-start | bytes 1769480 | tf_op jit(solution)/shard_map/ppermute | solution.py:79
  112.7 0.8 copy-start.16
  113.5 37.0 %collective-permute-start.24 = (bf16[512,1152]{1,0:T(8,128)(2,1)S(1)}, bf16[512,1152]{1,0:T(8,128)(2,1)}, u32[]{:S(2)}, u32[]{:S(2)}) collective-permute-start(bf16[512,1152]{1,0:T(8,128)(2,1)S(1)} %constant_dynamic-slice_fusion), channel_id=1, source_target_pairs={{8,0},{12,4},{0,8},{4,12},{24,16},{28,20},{16,24},{20,28},{9,1},{1... | collective-permute-start | bytes 3538952 | tf_op jit(solution)/shard_map/ppermute | solution.py:79
  115.0 58.4 %copy-start.12 = (bf16[576,512]{1,0:T(8,128)(2,1)}, bf16[576,512]{1,0:T(8,128)(2,1)S(1)}, u32[]{:S(2)}) copy-start(bf16[576,512]{1,0:T(8,128)(2,1)S(1)} %collective-permute-done.11.refs_2_) | copy-start | bytes 1769476
  115.0 58.4 %collective-permute-start.14 = (bf16[576,1024]{1,0:T(8,128)(2,1)S(1)}, bf16[576,1024]{1,0:T(8,128)(2,1)}, u32[]{:S(2)}, u32[]{:S(2)}) collective-permute-start(bf16[576,1024]{1,0:T(8,128)(2,1)S(1)} %collective-permute-done.13.refs_11_), channel_id=1, source_target_pairs={{16,0},{20,4},{24,8},{28,12},{0,16},{4,20},{8,24},{12,28},{17,1},{... | collective-permute-start | bytes 3538952 | tf_op jit(solution)/shard_map/ppermute | solution.py:79
  136.4 37.0 %collective-permute-start.18 = (bf16[512,1152]{1,0:T(8,128)(2,1)}, bf16[512,1152]{1,0:T(8,128)(2,1)}, u32[]{:S(2)}, u32[]{:S(2)}) collective-permute-start(bf16[512,1152]{1,0:T(8,128)(2,1)} %collective-permute-done.17.refs_15_), channel_id=1, source_target_pairs={{8,0},{12,4},{0,8},{4,12},{24,16},{28,20},{16,24},{20,28},{9,1},{1... | collective-permute-start | bytes 3538952 | tf_op jit(solution)/shard_map/ppermute | solution.py:79
  149.0 24.4 %copy-start.14 = (bf16[576,512]{1,0:T(8,128)(2,1)}, bf16[576,512]{1,0:T(8,128)(2,1)S(1)}, u32[]{:S(2)}) copy-start(bf16[576,512]{1,0:T(8,128)(2,1)S(1)} %collective-permute-done.8.refs_0_) | copy-start | bytes 1769476
  149.0 25.1 %collective-permute-start.21 = (bf16[576,1024]{1,0:T(8,128)(2,1)}, bf16[576,1024]{1,0:T(8,128)(2,1)}, u32[]{:S(2)}, u32[]{:S(2)}) collective-permute-start(bf16[576,1024]{1,0:T(8,128)(2,1)} %collective-permute-done.20.refs_0_), channel_id=1, source_target_pairs={{4,0},{0,4},{12,8},{8,12},{20,16},{16,20},{28,24},{24,28},{5,1},{1... | collective-permute-start | bytes 3538952 | tf_op jit(solution)/shard_map/ppermute | solution.py:79
  149.0 1.1 copy-start.4
  150.0 24.2 %collective-permute-start.34 = (bf16[512,1152]{1,0:T(8,128)(2,1)}, bf16[512,1152]{1,0:T(8,128)(2,1)}, u32[]{:S(2)}, u32[]{:S(2)}) collective-permute-start(bf16[512,1152]{1,0:T(8,128)(2,1)} %collective-permute-done.17.refs_15_), channel_id=1, source_target_pairs={{4,0},{0,4},{12,8},{8,12},{20,16},{16,20},{28,24},{24,28},{5,1},{1... | collective-permute-start | bytes 3538952 | tf_op jit(solution)/shard_map/ppermute | solution.py:79
  150.5 41.8 %collective-permute-start.25 = (bf16[512,1152]{1,0:T(8,128)(2,1)}, bf16[512,1152]{1,0:T(8,128)(2,1)}, u32[]{:S(2)}, u32[]{:S(2)}) collective-permute-start(bf16[512,1152]{1,0:T(8,128)(2,1)} %collective-permute-done.24.refs_4_), channel_id=1, source_target_pairs={{4,0},{0,4},{12,8},{8,12},{20,16},{16,20},{28,24},{24,28},{5,1},{1... | collective-permute-start | bytes 3538952 | tf_op jit(solution)/shard_map/ppermute | solution.py:79
  173.4 23.9 %collective-permute-start.15 = (bf16[576,1024]{1,0:T(8,128)(2,1)}, bf16[576,1024]{1,0:T(8,128)(2,1)}, u32[]{:S(2)}, u32[]{:S(2)}) collective-permute-start(bf16[576,1024]{1,0:T(8,128)(2,1)} %collective-permute-done.14.refs_0_), channel_id=1, source_target_pairs={{4,0},{0,4},{12,8},{8,12},{20,16},{16,20},{28,24},{24,28},{5,1},{1... | collective-permute-start | bytes 3538952 | tf_op jit(solution)/shard_map/ppermute | solution.py:79
  173.4 23.9 %collective-permute-start.19 = (bf16[512,1152]{1,0:T(8,128)(2,1)}, bf16[512,1152]{1,0:T(8,128)(2,1)}, u32[]{:S(2)}, u32[]{:S(2)}) collective-permute-start(bf16[512,1152]{1,0:T(8,128)(2,1)} %collective-permute-done.18.refs_2_), channel_id=1, source_target_pairs={{4,0},{0,4},{12,8},{8,12},{20,16},{16,20},{28,24},{24,28},{5,1},{1... | collective-permute-start | bytes 3538952 | tf_op jit(solution)/shard_map/ppermute | solution.py:79
  174.1 27.6 %collective-permute-start.12 = (bf16[576,512]{1,0:T(8,128)(2,1)}, bf16[576,512]{1,0:T(8,128)(2,1)}, u32[]{:S(2)}, u32[]{:S(2)}) collective-permute-start(bf16[576,512]{1,0:T(8,128)(2,1)} %copy-done.12), channel_id=1, source_target_pairs={{4,0},{0,4},{12,8},{8,12},{20,16},{16,20},{28,24},{24,28},{5,1},{1... | collective-permute-start | bytes 1769480 | tf_op jit(solution)/shard_map/ppermute | solution.py:79
  174.3 27.4 %collective-permute-start.9 = (bf16[576,512]{1,0:T(8,128)(2,1)}, bf16[576,512]{1,0:T(8,128)(2,1)}, u32[]{:S(2)}, u32[]{:S(2)}) collective-permute-start(bf16[576,512]{1,0:T(8,128)(2,1)} %copy-done.14), channel_id=1, source_target_pairs={{4,0},{0,4},{12,8},{8,12},{20,16},{16,20},{28,24},{24,28},{5,1},{1... | collective-permute-start | bytes 1769480 | tf_op jit(solution)/shard_map/ppermute | solution.py:79
  177.6 1.3 copy-start.3
  178.8 1.3 copy-start.5
  180.1 1.1 copy-start.7
  181.2 1.1 copy-start.9
  182.2 1.1 copy-start.11
  183.3 9.0 %copy-start.17 = (bf16[576,512]{1,0:T(8,128)(2,1)S(1)}, bf16[576,512]{1,0:T(8,128)(2,1)}, u32[]{:S(2)}) copy-start(bf16[576,512]{1,0:T(8,128)(2,1)} %copy-done.16) | copy-start | bytes 1769476
  197.3 4.3 %copy-start.13 = (bf16[576,512]{1,0:T(8,128)(2,1)S(1)}, bf16[576,512]{1,0:T(8,128)(2,1)}, u32[]{:S(2)}) copy-start(bf16[576,512]{1,0:T(8,128)(2,1)} %copy-done.12) | copy-start | bytes 1769476
  197.3 4.3 %copy-start.15 = (bf16[576,512]{1,0:T(8,128)(2,1)S(1)}, bf16[576,512]{1,0:T(8,128)(2,1)}, u32[]{:S(2)}) copy-start(bf16[576,512]{1,0:T(8,128)(2,1)} %copy-done.14) | copy-start | bytes 1769476
  201.7 3.1 %copy-start.1 = (bf16[1024,64]{0,1:T(8,128)(2,1)S(1)}, bf16[1024,64]{0,1:T(8,128)(2,1)}, u32[]{:S(2)}) copy-start(bf16[1024,64]{0,1:T(8,128)(2,1)} %param.24) | copy-start | bytes 393220
  (1 other events, 0.5 us)
